TPU v7x, 32 devices: a whole 2x2x4 slice. The times are simulated.
32 devices in a mesh: dp: 4 (over y, x), spatial: 8 (over z, core).
Axes of the slice: x: 2, y: 2, z: 4, core: 2. Of those that a mesh axis runs over, the one named last changes fastest.
Arguments:
- volume: bfloat16 [4, 16, 16, 8, 128], P('dp', 'spatial'), may hold values from -6 to 6
- cotangent: bfloat16 [4, 16, 16, 8, 128], P('dp', 'spatial'), may hold values from -6 to 6
- master: float32 [3456, 128], P('dp'), may hold values from -0.109375 to 0.109375
- moment: float32 [3456, 128], P('dp'), may hold values from -6 to 6
- second: float32 [3456, 128], P('dp'), may hold values from 0.25 to 4
Outputs:
- activation: bfloat16 [4, 16, 16, 8, 128], P('dp', 'spatial')
- input_grad: bfloat16 [4, 16, 16, 8, 128], P('dp', 'spatial')
- master_next: float32 [3456, 128], P('dp')
- moment_next: float32 [3456, 128], P('dp')
- second_next: float32 [3456, 128], P('dp')
All inputs are finite; a program needn't handle non-finite values.
Results may differ from a plain program's by a relative error of at most 0.002.
The roundings to bfloat16 on the way count: a program that leaves them out, or rounds other values in their place, can miss the bound.
Values may be sent and summed in bfloat16 or wider, within the bound.
A program may use at most 64 MiB of HBM per device.

v0:
```python
import math
import jax
import jax.numpy as jnp
from jax import lax
from jax.sharding import PartitionSpec as P


def with_halo(block, sides, width):
    for axis, dim in sides:
        count = lax.axis_size(axis)
        forward = [(i, i + 1) for i in range(count - 1)]
        backward = [(target, source) for source, target in forward]
        low = lax.ppermute(
            lax.slice_in_dim(block, block.shape[dim] - width, None, axis=dim), axis, forward
        )
        high = lax.ppermute(lax.slice_in_dim(block, 0, width, axis=dim), axis, backward)
        block = jnp.concatenate([low, block, high], axis=dim)
    return block


def silu_slope(preact):
    sigma = jax.nn.sigmoid(preact)
    return sigma * (1.0 + preact * (1.0 - sigma))


def pad_sides(field):
    return jnp.pad(field, ((0, 0), (1, 1), (1, 1), (0, 0)))


def forward_taps(padded, kernel, planes, rows, cols):
    width = kernel.shape[1]
    total = jnp.zeros((planes * rows * cols, width), jnp.float32)
    for offset_z in range(3):
        for offset_y in range(3):
            for offset_x in range(3):
                tap_index = offset_z * 9 + offset_y * 3 + offset_x
                piece = padded[
                    offset_z : offset_z + planes,
                    offset_y : offset_y + rows,
                    offset_x : offset_x + cols,
                ].reshape(-1, width)
                total = total + jnp.dot(
                    piece, kernel[tap_index], preferred_element_type=jnp.float32
                )
    return total


def backward_taps(grad_pad, kernel, planes, rows, cols):
    width = kernel.shape[1]
    total = jnp.zeros((planes * rows * cols, width), jnp.float32)
    for offset_z in range(3):
        for offset_y in range(3):
            for offset_x in range(3):
                tap_index = offset_z * 9 + offset_y * 3 + offset_x
                piece = grad_pad[
                    2 - offset_z : 2 - offset_z + planes,
                    2 - offset_y : 2 - offset_y + rows,
                    2 - offset_x : 2 - offset_x + cols,
                ].reshape(-1, width)
                total = total + lax.dot_general(
                    piece,
                    kernel[tap_index],
                    (((1,), (1,)), ((), ())),
                    preferred_element_type=jnp.float32,
                )
    return total


def weight_taps(padded, hidden_grad, planes, rows, cols):
    width = hidden_grad.shape[1]
    blocks = []
    for offset_z in range(3):
        for offset_y in range(3):
            for offset_x in range(3):
                piece = padded[
                    offset_z : offset_z + planes,
                    offset_y : offset_y + rows,
                    offset_x : offset_x + cols,
                ].reshape(-1, width)
                blocks.append(
                    lax.dot_general(
                        piece,
                        hidden_grad,
                        (((0,), (0,)), ((), ())),
                        preferred_element_type=jnp.float32,
                    )
                )
    return jnp.concatenate(blocks, axis=0)


def per_device(volume, cotangent, master, moment, second):
    planes = volume.shape[1]
    rows = volume.shape[2]
    cols = volume.shape[3]
    width = volume.shape[4]
    kernel = lax.all_gather(master.astype(jnp.bfloat16), "dp", axis=0, tiled=True).reshape(
        27, width, width
    )
    wide = with_halo(volume, (("spatial", 1),), 1)[0]
    padded = pad_sides(wide)
    preact = forward_taps(padded, kernel, planes, rows, cols)
    activated = jax.nn.silu(preact).astype(jnp.bfloat16)
    hidden_grad = (cotangent[0].reshape(-1, width).astype(jnp.float32) * silu_slope(preact)).astype(
        jnp.bfloat16
    )
    grad_block = hidden_grad.reshape(1, planes, rows, cols, width)
    wide_grad = with_halo(grad_block, (("spatial", 1),), 1)[0]
    grad_pad = pad_sides(wide_grad)
    input_grad = backward_taps(grad_pad, kernel, planes, rows, cols).astype(jnp.bfloat16)
    local_grad = weight_taps(padded, hidden_grad, planes, rows, cols)
    partial_grad = lax.psum_scatter(
        local_grad.astype(jnp.bfloat16), "dp", scatter_dimension=0, tiled=True
    ).astype(jnp.float32)
    shard = lax.psum(partial_grad, "spatial")
    cells_all = lax.axis_size("dp") * lax.axis_size("spatial") * planes * rows * cols
    weight_grad = shard / math.sqrt(cells_all)
    moment_next = 0.9 * moment + 0.1 * weight_grad
    second_next = 0.999 * second + 0.001 * weight_grad * weight_grad
    master_next = master - 0.001 * (moment_next / (jnp.sqrt(second_next) + 1e-08) + 0.01 * master)
    activation = activated.reshape(1, planes, rows, cols, width)
    input_block = input_grad.reshape(1, planes, rows, cols, width)
    return (activation, input_block, master_next, moment_next, second_next)


def solution(mesh):
    return jax.shard_map(
        per_device,
        mesh=mesh,
        in_specs=(
            P("dp", "spatial", None, None, None),
            P("dp", "spatial", None, None, None),
            P("dp", None),
            P("dp", None),
            P("dp", None),
        ),
        out_specs=(
            P("dp", "spatial", None, None, None),
            P("dp", "spatial", None, None, None),
            P("dp", None),
            P("dp", None),
            P("dp", None),
        ),
        check_vma=False,
    )
```

profile of v0, /device:TPU:0, one launch (start us, length us, event | category | flops | bytes accessed | tf_op | source)
XLA Modules:
  0.0 116.7 jit_solution(8562241958036103037)
XLA Ops:
  7.2 0.8 fusion.95
  8.0 2.4 %collective-permute-start = (bf16[1,1,16,8,128]{4,3,2,1,0:T(8,128)(2,1)S(1)}, bf16[1,1,16,8,128]{4,3,2,1,0:T(8,128)(2,1)S(1)}, u32[]{:S(2)}, u32[]{:S(2)}) collective-permute-start(bf16[1,1,16,8,128]{4,3,2,1,0:T(8,128)(2,1)S(1)} %get-tuple-element.64), channel_id=1, source_target_pairs={{0,1},{1,2},{2,3},{3,4},{4,5},{5,6},{6,7},{8,9},{9,10},{10,11},{11... | collective-permute-start | bytes 98312 | tf_op jit(solution)/shard_map/ppermute | solution.py:13
  10.4 1.3 %collective-permute-start.1 = (bf16[1,1,16,8,128]{4,3,2,1,0:T(8,128)(2,1)S(1)}, bf16[1,1,16,8,128]{4,3,2,1,0:T(8,128)(2,1)S(1)}, u32[]{:S(2)}, u32[]{:S(2)}) collective-permute-start(bf16[1,1,16,8,128]{4,3,2,1,0:T(8,128)(2,1)S(1)} %get-tuple-element.65), channel_id=1, source_target_pairs={{1,0},{2,1},{3,2},{4,3},{5,4},{6,5},{7,6},{9,8},{10,9},{11,10},{12... | collective-permute-start | bytes 98312 | tf_op jit(solution)/shard_map/ppermute | solution.py:16
  11.7 1.0 convert_element_type.25
  12.7 14.2 %all_gather.3 = bf16[3456,128]{1,0:T(8,128)(2,1)S(1)} all-gather(bf16[864,128]{1,0:T(8,128)(2,1)S(1)} %convert_element_type.25), channel_id=1, replica_groups=mesh['dp'=4,'spatial'=8] {'dp'}, dimensions={0}, use_global_device_ids=true | all-gather | bytes 1105920 | tf_op jit(solution)/shard_map/all_gather | solution.py:96
  27.0 0.2 pad_slice_fusion.24
  31.2 0.7 copy-done.5
  31.9 0.8 fusion.33
  32.7 0.2 fusion.30
  32.9 0.2 fusion.29
  33.1 0.2 fusion.28
  33.4 0.2 fusion.27
  33.6 0.2 fusion.26
  33.8 0.2 fusion.25
  34.0 0.2 fusion.24
  34.2 0.2 fusion.23
  34.4 0.2 fusion.22
  34.6 0.2 fusion.21
  34.8 0.2 fusion.20
  35.0 0.2 fusion.19
  35.2 0.2 fusion.18
  35.4 0.2 fusion.32
  35.7 0.2 fusion.17
  35.9 0.2 fusion.16
  36.1 0.2 fusion.15
  36.3 0.2 fusion.14
  36.5 0.2 fusion.13
  36.7 0.2 fusion.12
  36.9 0.2 fusion.11
  37.1 0.2 fusion.10
  37.3 0.2 fusion.9
  37.5 0.2 fusion.8
  37.8 0.2 fusion.7
  38.0 0.2 fusion.6
  38.2 2.4 %collective-permute-start.2 = (bf16[1,1,16,8,128]{4,3,2,1,0:T(8,128)(2,1)S(1)}, bf16[1,1,16,8,128]{4,3,2,1,0:T(8,128)(2,1)S(1)}, u32[]{:S(2)}, u32[]{:S(2)}) collective-permute-start(bf16[1,1,16,8,128]{4,3,2,1,0:T(8,128)(2,1)S(1)} %get-tuple-element.60), channel_id=1, source_target_pairs={{0,1},{1,2},{2,3},{3,4},{4,5},{5,6},{6,7},{8,9},{9,10},{10,11},{11... | collective-permute-start | bytes 98312 | tf_op jit(solution)/shard_map/ppermute | solution.py:13
  40.6 1.3 %collective-permute-start.3 = (bf16[1,1,16,8,128]{4,3,2,1,0:T(8,128)(2,1)S(1)}, bf16[1,1,16,8,128]{4,3,2,1,0:T(8,128)(2,1)S(1)}, u32[]{:S(2)}, u32[]{:S(2)}) collective-permute-start(bf16[1,1,16,8,128]{4,3,2,1,0:T(8,128)(2,1)S(1)} %get-tuple-element.61), channel_id=1, source_target_pairs={{1,0},{2,1},{3,2},{4,3},{5,4},{6,5},{7,6},{9,8},{10,9},{11,10},{12... | collective-permute-start | bytes 98312 | tf_op jit(solution)/shard_map/ppermute | solution.py:16
  41.9 0.2 fusion.5
  42.1 0.9 copy-done.2
  43.0 3.1 %collective-permute-done.3 = bf16[1,1,16,8,128]{4,3,2,1,0:T(8,128)(2,1)S(1)} collective-permute-done((bf16[1,1,16,8,128]{4,3,2,1,0:T(8,128)(2,1)S(1)}, bf16[1,1,16,8,128]{4,3,2,1,0:T(8,128)(2,1)S(1)}, u32[]{:S(2)}, u32[]{:S(2)}) %collective-permute-start.3) | collective-permute-done | bytes 32800 | tf_op jit(solution)/shard_map/ppermute | solution.py:16
  46.2 0.2 pad_slice_fusion
  46.8 0.2 convolution_add_fusion.23
  47.3 0.2 fusion.1
  49.8 0.2 convolution_add_fusion.6
  50.3 0.2 fusion
  50.9 0.8 fusion.4
  51.7 22.4 %reduce-scatter.2.cloned.1.call-done = bf16[864,128]{1,0:T(8,128)(2,1)} async-done(((bf16[3456,128]{1,0:T(8,128)(2,1)}), bf16[864,128]{1,0:T(8,128)(2,1)}) %reduce-scatter.2.cloned.1.call-update) | async-done | bytes 221200 | tf_op jit(solution)/shard_map/reduce_scatter | solution.py:111
  74.1 34.5 %all-reduce.3 = f32[864,128]{1,0:T(8,128)S(1)} all-reduce(bf16[864,128]{1,0:T(8,128)(2,1)} %reduce-scatter.2.cloned.1.call-done), channel_id=1, replica_groups=mesh['dp'=4,'spatial'=8] {'spatial'}, use_global_device_ids=true, to_apply=%region_1.2 | all-reduce | flops 110592 | bytes 663552 | tf_op jit(solution)/shard_map/psum | solution.py:114
  108.7 1.2 %multiply_subtract_fusion = (f32[864,128]{1,0:T(8,128)}, f32[864,128]{1,0:T(8,128)}, f32[864,128]{1,0:T(8,128)}) fusion(f32[864,128]{1,0:T(8,128)S(1)} %copy-done, f32[864,128]{1,0:T(8,128)S(1)} %all-reduce.3, f32[864,128]{1,0:T(8,128)S(1)} %copy-done.3, f32[864,128]{1,0:T(8,128)S(1)} %copy-done.4), kind=kLoop, calls=%fused_computation.156 | loop fusion | flops 1548288 | bytes 3096576 | tf_op jit(solution)/shard_map/sub | solution.py:119
  (70 shorter events, 7.7 us)
Async XLA Ops:
  7.2 66.9 %reduce-scatter.2.cloned.1.call-start = ((), (), s32[]{:S(2)}) async-start(), calls=%async_computation.1 | async-start | bytes 1105920 | tf_op jit(solution)/shard_map/reduce_scatter | solution.py:111
  8.0 18.9 %collective-permute-start = (bf16[1,1,16,8,128]{4,3,2,1,0:T(8,128)(2,1)S(1)}, bf16[1,1,16,8,128]{4,3,2,1,0:T(8,128)(2,1)S(1)}, u32[]{:S(2)}, u32[]{:S(2)}) collective-permute-start(bf16[1,1,16,8,128]{4,3,2,1,0:T(8,128)(2,1)S(1)} %get-tuple-element.64), channel_id=1, source_target_pairs={{0,1},{1,2},{2,3},{3,4},{4,5},{5,6},{6,7},{8,9},{9,10},{10,11},{11... | collective-permute-start | bytes 98312 | tf_op jit(solution)/shard_map/ppermute | solution.py:13
  10.4 16.5 %collective-permute-start.1 = (bf16[1,1,16,8,128]{4,3,2,1,0:T(8,128)(2,1)S(1)}, bf16[1,1,16,8,128]{4,3,2,1,0:T(8,128)(2,1)S(1)}, u32[]{:S(2)}, u32[]{:S(2)}) collective-permute-start(bf16[1,1,16,8,128]{4,3,2,1,0:T(8,128)(2,1)S(1)} %get-tuple-element.65), channel_id=1, source_target_pairs={{1,0},{2,1},{3,2},{4,3},{5,4},{6,5},{7,6},{9,8},{10,9},{11,10},{12... | collective-permute-start | bytes 98312 | tf_op jit(solution)/shard_map/ppermute | solution.py:16
  12.7 14.2 %copy-start.1 = (bf16[1,2,16,8,128]{4,3,2,1,0:T(8,128)(2,1)S(1)}, bf16[1,2,16,8,128]{4,3,2,1,0:T(8,128)(2,1)}, u32[]{:S(2)}) copy-start(bf16[1,2,16,8,128]{4,3,2,1,0:T(8,128)(2,1)} %param.5) | copy-start | bytes 196612
  31.1 0.8 copy-start.5
  38.2 4.8 %collective-permute-start.2 = (bf16[1,1,16,8,128]{4,3,2,1,0:T(8,128)(2,1)S(1)}, bf16[1,1,16,8,128]{4,3,2,1,0:T(8,128)(2,1)S(1)}, u32[]{:S(2)}, u32[]{:S(2)}) collective-permute-start(bf16[1,1,16,8,128]{4,3,2,1,0:T(8,128)(2,1)S(1)} %get-tuple-element.60), channel_id=1, source_target_pairs={{0,1},{1,2},{2,3},{3,4},{4,5},{5,6},{6,7},{8,9},{9,10},{10,11},{11... | collective-permute-start | bytes 98312 | tf_op jit(solution)/shard_map/ppermute | solution.py:13
  40.6 5.6 %collective-permute-start.3 = (bf16[1,1,16,8,128]{4,3,2,1,0:T(8,128)(2,1)S(1)}, bf16[1,1,16,8,128]{4,3,2,1,0:T(8,128)(2,1)S(1)}, u32[]{:S(2)}, u32[]{:S(2)}) collective-permute-start(bf16[1,1,16,8,128]{4,3,2,1,0:T(8,128)(2,1)S(1)} %get-tuple-element.61), channel_id=1, source_target_pairs={{1,0},{2,1},{3,2},{4,3},{5,4},{6,5},{7,6},{9,8},{10,9},{11,10},{12... | collective-permute-start | bytes 98312 | tf_op jit(solution)/shard_map/ppermute | solution.py:16
  42.1 0.9 copy-start.2
  50.5 58.1 %copy-start.4 = (f32[864,128]{1,0:T(8,128)S(1)}, f32[864,128]{1,0:T(8,128)}, u32[]{:S(2)}) copy-start(f32[864,128]{1,0:T(8,128)} %param.8) | copy-start | bytes 1327108
  50.9 57.8 %copy-start = (f32[864,128]{1,0:T(8,128)S(1)}, f32[864,128]{1,0:T(8,128)}, u32[]{:S(2)}) copy-start(f32[864,128]{1,0:T(8,128)} %param.7) | copy-start | bytes 1327108
  50.9 57.8 %copy-start.3 = (f32[864,128]{1,0:T(8,128)S(1)}, f32[864,128]{1,0:T(8,128)}, u32[]{:S(2)}) copy-start(f32[864,128]{1,0:T(8,128)} %param.9) | copy-start | bytes 1327108
Sparse Core Ops, SparseCore 0:
  43.1 30.9 reduce-scatter.1
where the time goes:
time: 117 us
  blocking collectives  48.7 us (42%)
  waiting for transfers between devices  25.6 us (22%)
  matrix products  15.3 us (13%)
  between operations  14.6 us (12%)
  starting transfers between devices  7.38 us (6%)
  local copies, waits for them, and re-layouts  2.93 us (3%)
  other arithmetic  2.34 us (2%)
    psum x1, blocking collectives, per_device(): shard = lax.psum(partial_grad, 'spatial')  34.5 us
    reduce_scatter x1, waiting for transfers between devices, per_device(): lax.psum_scatter(local_grad.astype(jnp.bfloat16), 'dp', scatter_dimension...  22.4 us
    all_gather x1, blocking collectives, per_device(): lax.all_gather(master.astype(jnp.bfloat16), 'dp', axis=0, tiled=True)  14.2 us
    dot_general x27, matrix products, weight_taps(): lax.dot_general(piece, hidden_grad, (((0,), (0,)), ((), ())), preferred_e...  5.53 us
    dot_general x27, matrix products, backward_taps(): lax.dot_general(piece, kernel[tap_index], (((1,), (1,)), ((), ())), prefe...  5.07 us
    ppermute x2, starting transfers between devices, with_halo(): lax.ppermute(lax.slice_in_dim(block, block.shape[dim] - width, None, axis...  4.76 us
    dot_general x27, matrix products, forward_taps(): jnp.dot(piece, kernel[tap_index], preferred_element_type=jnp.float32)  4.67 us
    ppermute x2, waiting for transfers between devices, with_halo(): lax.ppermute(lax.slice_in_dim(block, 0, width, axis=dim), axis, backward)  3.13 us
  transfers between devices with their start and end apart: 5, of which 2 were waited for; matrix products, arithmetic and copies ran while one was open for 6% of the time, Pallas kernels for 0%

commit v1 on v0

--- a/solution.py
+++ b/solution.py
@@ -111,7 +111,8 @@
     partial_grad = lax.psum_scatter(
         local_grad.astype(jnp.bfloat16), "dp", scatter_dimension=0, tiled=True
     ).astype(jnp.float32)
-    shard = lax.psum(partial_grad, "spatial")
+    shards = lax.all_gather(partial_grad, "spatial", axis=0, tiled=False)
+    shard = shards.sum(axis=0)
     cells_all = lax.axis_size("dp") * lax.axis_size("spatial") * planes * rows * cols
     weight_grad = shard / math.sqrt(cells_all)
     moment_next = 0.9 * moment + 0.1 * weight_grad

time: 117 us -> 123 us (1.051)
  blocking collectives: 48.7 us -> 15.7 us
  waiting for transfers between devices: 25.6 us -> 58.4 us
  other arithmetic: 2.34 us -> 7.12 us
  starting transfers between devices: 7.38 us -> 8.72 us
    all_gather x0 -> x1, waiting for transfers between devices: none -> 36.8 us  [per_device(): shards = lax.all_gather(partial_grad, 'spatial', axis=0, tiled=False)]
    psum x1 -> x0, blocking collectives: 34.5 us -> none  [per_device(): shard = lax.psum(partial_grad, 'spatial')]
    ppermute x2, waiting for transfers between devices: 3.13 us -> 0.01 us  [with_halo(): lax.ppermute(lax.slice_in_dim(block, 0, width, axis=dim), axis, backward)]
    reduce_sum x0 -> x1, other arithmetic: none -> 2.22 us  [per_device(): shard = shards.sum(axis=0)]
    all_gather x0 -> x1, other arithmetic: none -> 1.73 us  [per_device(): shards = lax.all_gather(partial_grad, 'spatial', axis=0, tiled=False)]
    reduce_scatter x1, waiting for transfers between devices: 22.4 us -> 20.8 us  [per_device(): lax.psum_scatter(local_grad.astype(jnp.bfloat16), 'dp', scatter_dimension...]
    all_gather x1, blocking collectives: 14.2 us -> 15.7 us  [per_device(): lax.all_gather(master.astype(jnp.bfloat16), 'dp', axis=0, tiled=True)]
    ppermute x2, starting transfers between devices: 4.76 us -> 6.06 us  [with_halo(): lax.ppermute(lax.slice_in_dim(block, block.shape[dim] - width, None, axis...]
  transfers between devices with their start and end apart: 5 -> 6, of which waited for: 2 -> 3; matrix products, arithmetic and copies ran while one was open for 6% -> 5% of each run, Pallas kernels for 0% -> 0%
where the time goes in v1:
time: 123 us; the launch traced here: 122 us
  waiting for transfers between devices  58.4 us (47%)
  blocking collectives  15.7 us (13%)
  matrix products  15.3 us (12%)
  between operations  14.6 us (12%)
  starting transfers between devices  8.72 us (7%)
  other arithmetic  7.12 us (6%)
  local copies, waits for them, and re-layouts  2.26 us (2%)
    all_gather x1, waiting for transfers between devices, per_device(): shards = lax.all_gather(partial_grad, 'spatial', axis=0, tiled=False)  36.8 us
    reduce_scatter x1, waiting for transfers between devices, per_device(): lax.psum_scatter(local_grad.astype(jnp.bfloat16), 'dp', scatter_dimension...  20.8 us
    all_gather x1, blocking collectives, per_device(): lax.all_gather(master.astype(jnp.bfloat16), 'dp', axis=0, tiled=True)  15.7 us
    ppermute x2, starting transfers between devices, with_halo(): lax.ppermute(lax.slice_in_dim(block, block.shape[dim] - width, None, axis...  6.06 us
    dot_general x27, matrix products, weight_taps(): lax.dot_general(piece, hidden_grad, (((0,), (0,)), ((), ())), preferred_e...  5.53 us
    dot_general x27, matrix products, backward_taps(): lax.dot_general(piece, kernel[tap_index], (((1,), (1,)), ((), ())), prefe...  5.07 us
    dot_general x27, matrix products, forward_taps(): jnp.dot(piece, kernel[tap_index], preferred_element_type=jnp.float32)  4.68 us
    ppermute x2, starting transfers between devices, with_halo(): lax.ppermute(lax.slice_in_dim(block, 0, width, axis=dim), axis, backward)  2.57 us
  transfers between devices with their start and end apart: 6, of which 3 were waited for; matrix products, arithmetic and copies ran while one was open for 5% of the time, Pallas kernels for 0%

profile of v1, /device:TPU:0, one launch (start us, length us, event | category | flops | bytes accessed | tf_op | source)
XLA Modules:
  0.0 122.1 jit_solution(16091689794086015704)
XLA Ops:
  7.2 0.8 fusion.95
  8.0 1.3 %collective-permute-start.1 = (bf16[1,1,16,8,128]{4,3,2,1,0:T(8,128)(2,1)S(1)}, bf16[1,1,16,8,128]{4,3,2,1,0:T(8,128)(2,1)S(1)}, u32[]{:S(2)}, u32[]{:S(2)}) collective-permute-start(bf16[1,1,16,8,128]{4,3,2,1,0:T(8,128)(2,1)S(1)} %get-tuple-element.65), channel_id=1, source_target_pairs={{1,0},{2,1},{3,2},{4,3},{5,4},{6,5},{7,6},{9,8},{10,9},{11,10},{12... | collective-permute-start | bytes 98312 | tf_op jit(solution)/shard_map/ppermute | solution.py:16
  9.3 3.0 %collective-permute-start = (bf16[1,1,16,8,128]{4,3,2,1,0:T(8,128)(2,1)S(1)}, bf16[1,1,16,8,128]{4,3,2,1,0:T(8,128)(2,1)S(1)}, u32[]{:S(2)}, u32[]{:S(2)}) collective-permute-start(bf16[1,1,16,8,128]{4,3,2,1,0:T(8,128)(2,1)S(1)} %get-tuple-element.64), channel_id=1, source_target_pairs={{0,1},{1,2},{2,3},{3,4},{4,5},{5,6},{6,7},{8,9},{9,10},{10,11},{11... | collective-permute-start | bytes 98312 | tf_op jit(solution)/shard_map/ppermute | solution.py:13
  12.3 1.0 convert_element_type.23
  13.4 15.7 %all_gather.12 = bf16[3456,128]{1,0:T(8,128)(2,1)S(1)} all-gather(bf16[864,128]{1,0:T(8,128)(2,1)S(1)} %convert_element_type.23), channel_id=1, replica_groups=mesh['dp'=4,'spatial'=8] {'dp'}, dimensions={0}, use_global_device_ids=true | all-gather | bytes 1105920 | tf_op jit(solution)/shard_map/all_gather | solution.py:96
  29.1 0.9 maximum_bitcast_fusion
  30.0 0.2 pad_slice_fusion.24
  34.3 0.8 fusion.33
  35.1 0.2 fusion.30
  35.3 0.2 fusion.29
  35.5 0.2 fusion.28
  35.7 0.2 fusion.27
  35.9 0.2 fusion.26
  36.1 0.2 fusion.25
  36.4 0.2 fusion.24
  36.6 0.2 fusion.23
  36.8 0.2 fusion.22
  37.0 0.2 fusion.21
  37.2 0.2 fusion.20
  37.4 0.2 fusion.19
  37.6 0.2 fusion.18
  37.8 0.2 fusion.32
  38.0 0.2 fusion.17
  38.3 0.2 fusion.16
  38.5 0.2 fusion.15
  38.7 0.2 fusion.14
  38.9 0.2 fusion.13
  39.1 0.2 fusion.12
  39.3 0.2 fusion.11
  39.5 0.2 fusion.10
  39.7 0.2 fusion.9
  39.9 0.2 fusion.8
  40.1 0.2 fusion.7
  40.3 0.2 fusion.6
  40.5 0.2 fusion.5
  40.8 0.9 copy-done.2
  41.8 1.3 %collective-permute-start.3 = (bf16[1,1,16,8,128]{4,3,2,1,0:T(8,128)(2,1)S(1)}, bf16[1,1,16,8,128]{4,3,2,1,0:T(8,128)(2,1)S(1)}, u32[]{:S(2)}, u32[]{:S(2)}) collective-permute-start(bf16[1,1,16,8,128]{4,3,2,1,0:T(8,128)(2,1)S(1)} %get-tuple-element.61), channel_id=1, source_target_pairs={{1,0},{2,1},{3,2},{4,3},{5,4},{6,5},{7,6},{9,8},{10,9},{11,10},{12... | collective-permute-start | bytes 98312 | tf_op jit(solution)/shard_map/ppermute | solution.py:16
  43.1 3.0 %collective-permute-start.2 = (bf16[1,1,16,8,128]{4,3,2,1,0:T(8,128)(2,1)S(1)}, bf16[1,1,16,8,128]{4,3,2,1,0:T(8,128)(2,1)S(1)}, u32[]{:S(2)}, u32[]{:S(2)}) collective-permute-start(bf16[1,1,16,8,128]{4,3,2,1,0:T(8,128)(2,1)S(1)} %get-tuple-element.60), channel_id=1, source_target_pairs={{0,1},{1,2},{2,3},{3,4},{4,5},{5,6},{6,7},{8,9},{9,10},{10,11},{11... | collective-permute-start | bytes 98312 | tf_op jit(solution)/shard_map/ppermute | solution.py:13
  46.1 0.8 collective-permute-done.2
  47.2 20.8 %reduce-scatter.2.cloned.1.call-done = bf16[864,128]{1,0:T(8,128)(2,1)} async-done(((bf16[3456,128]{1,0:T(8,128)(2,1)}), bf16[864,128]{1,0:T(8,128)(2,1)}) %reduce-scatter.2.cloned.1.call-update) | async-done | bytes 221200 | tf_op jit(solution)/shard_map/reduce_scatter | solution.py:111
  68.0 1.7 %all_gather.16 = f32[864,128]{1,0:T(8,128)} convert(bf16[864,128]{1,0:T(8,128)(2,1)} %reduce-scatter.2.cloned.1.call-done) | non-fusion elementwise | flops 110592 | bytes 663552 | tf_op jit(solution)/shard_map/all_gather | solution.py:114
  69.8 0.2 pad_slice_fusion
  70.3 0.2 convolution_add_fusion.23
  73.9 0.2 convolution_add_fusion.2
  74.2 0.8 fusion.4
  75.0 36.8 %all-gather.3.cloned.1.call-done = f32[6912,128]{1,0:T(8,128)} async-done(((f32[864,128]{1,0:T(8,128)}), f32[6912,128]{1,0:T(8,128)}) %all-gather.3.cloned.1.call-update) | async-done | bytes 3538960 | tf_op jit(solution)/shard_map/all_gather | solution.py:114
  111.8 2.2 %reduce_sum.9 = f32[864,128]{1,0:T(8,128)S(1)} reduce(f32[8,864,128]{2,1,0:T(8,128)} %bitcast.179, f32[]{:T(128)} %constant.8.clone.1), dimensions={0}, to_apply=%region_1.2 | reduce | flops 774144 | bytes 3981316 | tf_op jit(solution)/shard_map/reduce_sum | solution.py:115
  114.0 1.2 %multiply_subtract_fusion = (f32[864,128]{1,0:T(8,128)}, f32[864,128]{1,0:T(8,128)}, f32[864,128]{1,0:T(8,128)}) fusion(f32[864,128]{1,0:T(8,128)S(1)} %copy-done, f32[864,128]{1,0:T(8,128)S(1)} %reduce_sum.9, f32[864,128]{1,0:T(8,128)S(1)} %copy-done.3, f32[864,128]{1,0:T(8,128)S(1)} %copy-done.4), kind=kLoop, calls=%fused_computation.156 | loop fusion | flops 1548288 | bytes 3096576 | tf_op jit(solution)/shard_map/sub | solution.py:120
  (74 shorter events, 8.1 us)
Async XLA Ops:
  7.2 24.0 %copy-start.1 = (bf16[1,2,16,8,128]{4,3,2,1,0:T(8,128)(2,1)S(1)}, bf16[1,2,16,8,128]{4,3,2,1,0:T(8,128)(2,1)}, u32[]{:S(2)}) copy-start(bf16[1,2,16,8,128]{4,3,2,1,0:T(8,128)(2,1)} %param.5) | copy-start | bytes 196612
  7.2 60.8 %reduce-scatter.2.cloned.1.call-start = ((), (), s32[]{:S(2)}) async-start(), calls=%async_computation.1 | async-start | bytes 1105920 | tf_op jit(solution)/shard_map/reduce_scatter | solution.py:111
  8.0 21.1 %collective-permute-start.1 = (bf16[1,1,16,8,128]{4,3,2,1,0:T(8,128)(2,1)S(1)}, bf16[1,1,16,8,128]{4,3,2,1,0:T(8,128)(2,1)S(1)}, u32[]{:S(2)}, u32[]{:S(2)}) collective-permute-start(bf16[1,1,16,8,128]{4,3,2,1,0:T(8,128)(2,1)S(1)} %get-tuple-element.65), channel_id=1, source_target_pairs={{1,0},{2,1},{3,2},{4,3},{5,4},{6,5},{7,6},{9,8},{10,9},{11,10},{12... | collective-permute-start | bytes 98312 | tf_op jit(solution)/shard_map/ppermute | solution.py:16
  9.3 19.8 %collective-permute-start = (bf16[1,1,16,8,128]{4,3,2,1,0:T(8,128)(2,1)S(1)}, bf16[1,1,16,8,128]{4,3,2,1,0:T(8,128)(2,1)S(1)}, u32[]{:S(2)}, u32[]{:S(2)}) collective-permute-start(bf16[1,1,16,8,128]{4,3,2,1,0:T(8,128)(2,1)S(1)} %get-tuple-element.64), channel_id=1, source_target_pairs={{0,1},{1,2},{2,3},{3,4},{4,5},{5,6},{6,7},{8,9},{9,10},{10,11},{11... | collective-permute-start | bytes 98312 | tf_op jit(solution)/shard_map/ppermute | solution.py:13
  31.4 2.9 %copy-start.5 = (bf16[1,2,16,8,128]{4,3,2,1,0:T(8,128)(2,1)S(1)}, bf16[1,2,16,8,128]{4,3,2,1,0:T(8,128)(2,1)}, u32[]{:S(2)}) copy-start(bf16[1,2,16,8,128]{4,3,2,1,0:T(8,128)(2,1)} %param.6) | copy-start | bytes 196612
  40.8 0.9 copy-start.2
  41.7 70.1 %all-gather.3.cloned.1.call-start = ((), (), s32[]{:S(2)}) async-start(), calls=%async_computation.2 | async-start | bytes 3981312 | tf_op jit(solution)/shard_map/all_gather | solution.py:114
  41.8 4.3 %collective-permute-start.3 = (bf16[1,1,16,8,128]{4,3,2,1,0:T(8,128)(2,1)S(1)}, bf16[1,1,16,8,128]{4,3,2,1,0:T(8,128)(2,1)S(1)}, u32[]{:S(2)}, u32[]{:S(2)}) collective-permute-start(bf16[1,1,16,8,128]{4,3,2,1,0:T(8,128)(2,1)S(1)} %get-tuple-element.61), channel_id=1, source_target_pairs={{1,0},{2,1},{3,2},{4,3},{5,4},{6,5},{7,6},{9,8},{10,9},{11,10},{12... | collective-permute-start | bytes 98312 | tf_op jit(solution)/shard_map/ppermute | solution.py:16
  43.1 3.9 %collective-permute-start.2 = (bf16[1,1,16,8,128]{4,3,2,1,0:T(8,128)(2,1)S(1)}, bf16[1,1,16,8,128]{4,3,2,1,0:T(8,128)(2,1)S(1)}, u32[]{:S(2)}, u32[]{:S(2)}) collective-permute-start(bf16[1,1,16,8,128]{4,3,2,1,0:T(8,128)(2,1)S(1)} %get-tuple-element.60), channel_id=1, source_target_pairs={{0,1},{1,2},{2,3},{3,4},{4,5},{5,6},{6,7},{8,9},{9,10},{10,11},{11... | collective-permute-start | bytes 98312 | tf_op jit(solution)/shard_map/ppermute | solution.py:13
  73.0 41.0 %copy-start = (f32[864,128]{1,0:T(8,128)S(1)}, f32[864,128]{1,0:T(8,128)}, u32[]{:S(2)}) copy-start(f32[864,128]{1,0:T(8,128)} %param.7) | copy-start | bytes 1327108
  73.0 41.0 %copy-start.3 = (f32[864,128]{1,0:T(8,128)S(1)}, f32[864,128]{1,0:T(8,128)}, u32[]{:S(2)}) copy-start(f32[864,128]{1,0:T(8,128)} %param.9) | copy-start | bytes 1327108
  73.0 41.0 %copy-start.4 = (f32[864,128]{1,0:T(8,128)S(1)}, f32[864,128]{1,0:T(8,128)}, u32[]{:S(2)}) copy-start(f32[864,128]{1,0:T(8,128)} %param.8) | copy-start | bytes 1327108
Sparse Core Ops, SparseCore 0:
  41.8 26.1 reduce-scatter.1
  70.2 41.5 all-gather.2
